TPU v7x, 128 devices: a whole 4x4x4 slice. The times are simulated.
128 devices in a mesh: freq: 2 (over core), dir: 4 (over y), ap: 16 (over z, x).
Axes of the slice: x: 4, y: 4, z: 4, core: 2. Of those that a mesh axis runs over, the one named last changes fastest.
Arguments:
- signal: bfloat16 [2, 65536, 2048], P(None, 'ap', ('freq', 'dir')), parts along dimension 2, may hold values from -6 to 6
- positions: int32 [2, 65536], P(None, 'ap'), may hold values from 0 to 255
- weights: bfloat16 [4, 2, 2, 2, 256, 256], replicated, may hold values from -0.1875 to 0.1875
- directions: int32 [2, 16, 4096], P(None, 'ap', 'dir'), may hold values from 0 to 255
Outputs:
- beams: bfloat16 [2, 16, 4096, 2048], P(None, 'ap', 'dir', 'freq'), parts along dimension 3
There are 2 independent parts, one for each index of `freq`. A program takes and returns all parts, laid end to end along the dimension named above; an argument that names none is the same for every part. Nothing has to cross between parts.
All inputs are finite; a program needn't handle non-finite values.
Results may differ from a plain program's by a relative error of at most 0.009.
Values may be sent and summed in bfloat16 or wider, within the bound.
No kernel may reach another device: no remote copies, remote signals or barrier semaphores. Data moves between devices by JAX's collectives and lax.ppermute only.
A program may use at most 128 MiB of HBM per device.

v0:
```python
import math

import jax
import jax.numpy as jnp
from jax import lax
from jax.experimental import pallas as pl
from jax.experimental.pallas import tpu as pltpu
from jax.sharding import Mesh, PartitionSpec as P


K = 256
EB = 256
SIDE = 16
BOXES = 16
COLS = 256
F32 = jnp.float32
BF = jnp.bfloat16

LEAD_MIB = 34


def sincos(phase):
    p = jnp.bitwise_and(phase, 255)
    q = jnp.right_shift(p + 32, 6)
    t = (p - jnp.left_shift(q, 6)).astype(F32) * (2.0 * math.pi / 256.0)
    u = t * t
    s0 = t * (1.0 + u * (-1.0 / 6 + u * (1.0 / 120 + u * (-1.0 / 5040 + u * (1.0 / 362880)))))
    c0 = 1.0 + u * (-0.5 + u * (1.0 / 24 + u * (-1.0 / 720 + u * (1.0 / 40320))))
    odd = jnp.bitwise_and(q, 1) == 1
    c = jnp.where(odd, s0, c0)
    s = jnp.where(odd, c0, s0)
    c = jnp.where(jnp.bitwise_and(q + 1, 2) == 2, -c, c)
    s = jnp.where(jnp.bitwise_and(q, 2) == 2, -s, s)
    return c, s


def dot(a, b):
    return jnp.dot(a, b, preferred_element_type=F32)


OFFSETS = (2, 1, 3, 0)


def composites(mm, w43, e21, slots):
    core = lax.axis_index("freq")
    own_z, own_x = lax.axis_index("z"), lax.axis_index("x")
    for i, slot in enumerate(slots):
        major, minor = OFFSETS[slot // 4], OFFSETS[slot % 4]
        z = jnp.bitwise_and(own_z + jnp.where(core == 0, major, minor), 3)
        x = jnp.bitwise_and(own_x + jnp.where(core == 0, minor, major), 3)
        left = w43[pl.ds(pl.multiple_of(x * K, K), K), :]
        mm[:, i] = dot(left, e21[z]).astype(BF).reshape(16, 16, 2 * K)


def dft4(x):
    (a, b), (c, d), (e, f), (g, h) = x
    s0r, s0i, d0r, d0i = a + e, b + f, a - e, b - f
    s1r, s1i, d1r, d1i = c + g, d + h, c - g, d - h
    return (
        (s0r + s1r, s0i + s1i),
        (d0r + d1i, d0i - d1r),
        (s0r - s1r, s0i - s1i),
        (d0r - d1i, d0i + d1r),
    )


def expand_right(row_form):
    n = row_form.shape[-1] // 2
    r, i = row_form[:, :n], row_form[:, n:]
    return jnp.concatenate(
        [jnp.concatenate([r, i], 1), jnp.concatenate([-i, r], 1)], 0
    )


VMEM = pltpu.VMEM


def lead_kernel(pos_hbm, sig_hbm, w_hbm, *rest):
    p2hi, p2lo, d, w43, e21 = rest[:5]
    pos, sig, w, ax_c, ax_s, by_c, by_s, t0, t1, c0, mm, wsem, ssem = rest[5:]
    own_z, own_x = lax.axis_index("z"), lax.axis_index("x")
    child = (own_z // 2, own_z % 2, own_x // 2, own_x % 2)

    pos_copy = pltpu.make_async_copy(pos_hbm, pos, wsem.at[4])
    pos_copy.start()
    w_copies = [
        pltpu.make_async_copy(w_hbm.at[i, :, child[i]], w.at[i], wsem.at[i])
        for i in range(4)
    ]
    for i in (3, 2, 1, 0):
        w_copies[i].start()
    quarter = sig.shape[1] // 4
    s_copies = [
        pltpu.make_async_copy(
            sig_hbm.at[:, pl.ds(i * quarter, quarter), :],
            sig.at[:, pl.ds(i * quarter, quarter), :],
            ssem.at[i],
        )
        for i in range(4)
    ]
    for c in s_copies:
        c.start()

    pos_copy.wait()
    wave = lax.broadcasted_iota(jnp.int32, (SIDE, 1), 0) - SIDE // 2

    def factors(i, _):
        lanes = pl.ds(pl.multiple_of(i * 512, 512), 512)
        xc, xs = sincos(wave * pos[0:1, lanes])
        ax_c[:, lanes] = xc * (1.0 / 16.0)
        ax_s[:, lanes] = xs * (1.0 / 16.0)
        yc, ys = sincos(wave * pos[1:2, lanes])
        by_c[:, lanes] = yc
        by_s[:, lanes] = ys
        return 0

    lax.fori_loop(0, pos.shape[1] // 512, factors, 0)

    row = lax.broadcasted_iota(jnp.int32, (K, K), 0)
    col = lax.broadcasted_iota(jnp.int32, (K, K), 1)
    kx, ky = row // 64, row // 16 % 4
    hx, hy = row // 4 % 4, row % 4
    source = (hx * 4 + kx) * 16 + hy * 4 + ky
    pick = jnp.where(source == col, 1.0, 0.0).astype(BF)

    def row_form(level, r):
        return jnp.concatenate([w[level, r, 0], w[level, r, 1]], 1)

    w_copies[3].wait()
    upper = jnp.concatenate(
        [dot(pick, row_form(3, r)).astype(BF) for r in range(2)], 0
    )
    w_copies[2].wait()
    for r3 in range(2):
        w43[pl.ds(r3 * 512, 512), :] = dot(upper, expand_right(row_form(2, r3))).astype(BF)
    w_copies[1].wait()
    w_copies[0].wait()
    lower = jnp.concatenate([row_form(1, r) for r in range(2)], 0)
    for r1 in range(2):
        both = dot(lower, expand_right(row_form(0, r1))).astype(BF)
        for r2 in range(2):
            e21[r1 * 2 + r2] = expand_right(both[r2 * K : (r2 + 1) * K])

    composites(mm, w43, e21, range(4))

    def build(table, m):
        lanes = slice(m * EB, (m + 1) * EB)
        bc, bs = by_c[:, lanes], by_s[:, lanes]
        for wx in range(SIDE):
            ac, as_ = ax_c[wx : wx + 1, lanes], ax_s[wx : wx + 1, lanes]
            table[wx * 16 : wx * 16 + 16, 0:EB] = (ac * bc - as_ * bs).astype(BF)
            table[wx * 16 : wx * 16 + 16, EB : 2 * EB] = (as_ * bc + ac * bs).astype(BF)

    def multiply(table, m):
        sr = sig[0, m * EB : (m + 1) * EB, :]
        si = sig[1, m * EB : (m + 1) * EB, :]
        right = jnp.concatenate(
            [jnp.concatenate([sr, si], 1), jnp.concatenate([si, -sr], 1)], 0
        )
        c0[m] = dot(table[...], right)

    def along_x(my, part):
        for i in range(part * 8, part * 8 + 8):
            rows = slice(i * 8, i * 8 + 8)
            for half in range(2):
                re_at = slice(half * 128, half * 128 + 128)
                im_at = slice(COLS + half * 128, COLS + half * 128 + 128)
                x = [
                    (c0[my * 4 + mx, rows, re_at], c0[my * 4 + mx, rows, im_at])
                    for mx in range(4)
                ]
                for kx_, (re, im) in enumerate(dft4(x)):
                    c0[my * 4 + kx_, rows, re_at] = re
                    c0[my * 4 + kx_, rows, im_at] = im

    def along_y(kx_, part):
        for i in range(part * 4, part * 4 + 4):
            rows = slice(i * 16, i * 16 + 16)
            low = slice(K + i * 16, K + i * 16 + 16)
            for half in range(2):
                re_at = slice(half * 128, half * 128 + 128)
                im_at = slice(COLS + half * 128, COLS + half * 128 + 128)
                x = [
                    (c0[my * 4 + kx_, rows, re_at], c0[my * 4 + kx_, rows, im_at])
                    for my in range(4)
                ]
                for ky_, (re, im) in enumerate(dft4(x)):
                    re = (re * 0.25).astype(BF)
                    im = (im * 0.25).astype(BF)
                    cls = kx_ * 4 + ky_
                    d[cls, rows, re_at] = re
                    d[cls, rows, im_at] = im
                    d[cls, low, re_at] = -im
                    d[cls, low, im_at] = re

    def apply(cls):
        rows = slice(cls * 16, cls * 16 + 16)
        out = dot(mm[cls].reshape(K // 4, 2 * K), d[cls]).astype(BF).reshape(4, 16, 2 * COLS)
        p2hi[:, rows, :] = out[0:2]
        p2lo[:, rows, :] = out[2:4]

    tables = (t0, t1)
    build(t0, 0)
    for m in range(BOXES):
        if m % 4 == 0:
            s_copies[m // 4].wait()
        if m + 1 < BOXES:
            build(tables[(m + 1) % 2], m + 1)
        multiply(tables[m % 2], m)
        if m >= 4:
            along_x(m // 4 - 1, m % 4)
    for part in range(4):
        along_x(3, part)
    for part in range(4):
        along_y(0, part)
    for cls in range(16):
        if cls < 12:
            along_y(cls // 4 + 1, cls % 4)
        apply(cls)


def vm(n):
    return [pl.BlockSpec(memory_space=VMEM)] * n


def shaped(*dims, dtype=BF):
    return jax.ShapeDtypeStruct(dims, dtype)


def rest_kernel(d, w43, e21, *refs):
    q1f, q1n, qmf, qmn, own, mm = refs
    composites(mm, w43, e21, range(4, 16))
    for cls in range(16):
        rows = slice(cls * 16, cls * 16 + 16)
        out = dot(mm[cls].reshape(3 * K // 4, 2 * K), d[cls]).astype(BF)
        out = out.reshape(3, 4, 16, 2 * COLS)
        q1f[rows, :] = out[0, 0]
        q1n[:, rows, :] = out[0, 1:4]
        qmf[rows, :] = out[1, 0]
        qmn[:, rows, :] = out[1, 1:4]
        own[:, rows, :] = out[2]


def lead(positions, signal, weights):
    ne = positions.shape[1]
    hbm = pl.BlockSpec(memory_space=pltpu.HBM)
    far = pl.pallas_call(
        lead_kernel,
        out_shape=[shaped(2, K, 2 * COLS)] * 2
        + [shaped(16, 2 * K, 2 * COLS), shaped(4 * K, 2 * K), shaped(4, 2 * K, 2 * K)],
        in_specs=[hbm] * 3,
        out_specs=vm(5),
        scratch_shapes=[
            VMEM(positions.shape, jnp.int32),
            VMEM(signal.shape, BF),
            VMEM((4, 2, 2, K, K), BF),
        ]
        + [VMEM((SIDE, ne), F32)] * 4
        + [VMEM((K, 2 * EB), BF)] * 2
        + [
            VMEM((BOXES, K, 2 * COLS), F32),
            VMEM((16, 4, 16, 2 * K), BF),
            pltpu.SemaphoreType.DMA((5,)),
            pltpu.SemaphoreType.DMA((4,)),
        ],
        compiler_params=pltpu.CompilerParams(vmem_limit_bytes=LEAD_MIB << 20),
        cost_estimate=pl.CostEstimate(
            flops=8_000_000_000, transcendentals=0, bytes_accessed=12 << 20
        ),
        name="lead",
    )(*(pltpu.with_memory_space_constraint(a, pltpu.HBM) for a in (positions, signal, weights)))
    p2hi, p2lo, d, w43, e21 = far
    near = pl.pallas_call(
        rest_kernel,
        out_shape=[
            shaped(*n, K, 2 * COLS) for n in ((), (3,), (), (3,), (4,))
        ],
        in_specs=vm(3),
        out_specs=vm(5),
        scratch_shapes=[VMEM((16, 12, 16, 2 * K), BF)],
        compiler_params=pltpu.CompilerParams(vmem_limit_bytes=30 << 20),
        cost_estimate=pl.CostEstimate(
            flops=3_000_000_000, transcendentals=0, bytes_accessed=12 << 20
        ),
        name="rest",
    )(d, w43, e21)
    return p2hi, p2lo, *near


def steer_kernel(pos, out, table):
    r = lax.broadcasted_iota(jnp.int32, (SIDE, 1), 0)
    n = pos.shape[-1]
    u, v = pos[0, 0:1, :], pos[1, 0:1, :]
    for kx in range(4):
        ac, as_ = sincos((r // 4 * 4 + kx - 8) * u)
        ac, as_ = ac * (1.0 / 16.0), as_ * (1.0 / 16.0)
        for ky in range(4):
            bc, bs = sincos((r % 4 * 4 + ky - 8) * v)
            rows = pl.ds((kx * 4 + ky) * 16, 16)
            table[rows, :] = ac * bc - as_ * bs
            table[pl.ds((kx * 4 + ky) * 16 + K, 16), :] = as_ * bc + ac * bs
    for i in range(n // 128):
        for j in range(2 * K // 128):
            block = table[pl.ds(j * 128, 128), pl.ds(i * 128, 128)]
            out[pl.ds(i * 128, 128), pl.ds(j * 128, 128)] = block.T.astype(BF)


def steer(directions):
    n = directions.shape[-1]
    return pl.pallas_call(
        steer_kernel,
        out_shape=shaped(n, 2 * K),
        in_specs=vm(1),
        out_specs=vm(1)[0],
        scratch_shapes=[VMEM((2 * K, n), F32)],
        cost_estimate=pl.CostEstimate(
            flops=1_500_000_000, transcendentals=0, bytes_accessed=1 << 20
        ),
        compiler_params=pltpu.CompilerParams(vmem_limit_bytes=16 << 20),
        name="steer",
    )(directions)


def added(*terms):
    total = terms[0].astype(F32)
    for t in terms[1:]:
        total = total + t.astype(F32)
    return total


def call(kernel, shapes, *args):
    return pl.pallas_call(
        kernel,
        out_shape=shapes,
        in_specs=vm(len(args)),
        out_specs=vm(len(shapes)),
        compiler_params=pltpu.CompilerParams(vmem_limit_bytes=24 << 20),
    )(*args)


def merge_down_kernel(far, near, received, out_far, out_near):
    out_far[...] = added(far[...], received[0]).astype(BF)
    out_near[0] = added(near[0], received[1]).astype(BF)
    out_near[1:3] = near[1:3]


def merge_up_kernel(near, received, out_near):
    out_near[0] = near[0]
    out_near[1:3] = added(near[1:3], received[...]).astype(BF)


def sum_far_kernel(own, up, down, out):
    out[...] = added(own[0], up[...], down[...]).astype(BF)


def sum_near_kernel(own, up, down, u1, um, s0):
    u1[...] = added(own[1], up[0], down[0]).astype(BF)
    um[...] = added(own[2], up[1], down[1]).astype(BF)
    s0[...] = added(own[3], up[2], down[2])


def total_kernel(s0, t2, v1, v_m, z):
    z[...] = added(s0[...], t2[...], v1[...], v_m[...]).astype(BF)


def beam_kernel(offsets, table, *rest):
    parts = rest[: len(offsets)]
    out, buf, sem = rest[-3:]
    y = lax.axis_index("dir")
    n = table.shape[0] // 2
    copies = []
    for i, offset in enumerate(offsets):
        right = expand_right(parts[i][...])
        column = pl.multiple_of(jnp.bitwise_and(y + offset, 3) * COLS, COLS)
        for r in range(2):
            slot = len(copies) % 2
            if len(copies) >= 2:
                copies[-2].wait()
            b = dot(table[pl.ds(r * n, n), :], right).astype(BF)
            buf[slot, 0] = b[:, :COLS]
            buf[slot, 1] = b[:, COLS:]
            copies.append(
                pltpu.make_async_copy(
                    buf.at[slot],
                    out.at[:, 0, pl.ds(r * n, n), pl.ds(column, COLS)],
                    sem.at[slot],
                )
            )
            copies[-1].start()
    for c in copies[-2:]:
        c.wait()


def beams(offsets, table, parts, previous, shape):
    n = table.shape[0]
    hbm = pl.BlockSpec(memory_space=pltpu.HBM)
    extra = [] if previous is None else [previous]
    return pl.pallas_call(
        lambda *refs: beam_kernel(offsets, *refs),
        out_shape=jax.ShapeDtypeStruct(shape, BF),
        in_specs=vm(1 + len(parts)) + [hbm] * len(extra),
        out_specs=hbm,
        scratch_shapes=[
            VMEM((2, 2, n // 2, COLS), BF),
            pltpu.SemaphoreType.DMA((2,)),
        ],
        input_output_aliases={} if previous is None else {1 + len(parts): 0},
        cost_estimate=pl.CostEstimate(
            flops=2_000_000_000, transcendentals=0, bytes_accessed=1 << 20
        ),
        compiler_params=pltpu.CompilerParams(vmem_limit_bytes=24 << 20),
        name="beams",
    )(table, *parts, *extra)


def ring(step, first):
    pairs = []
    for z in range(4):
        for x in range(4):
            along_z = ((z + step) % 4) * 4 + x
            along_x = z * 4 + (x + step) % 4
            core0, core1 = (along_z, along_x) if first else (along_x, along_z)
            pairs.append((z * 4 + x, core0))
            pairs.append((16 + z * 4 + x, 16 + core1))
    return pairs


def local(signal, positions, weights, directions):
    along = ("freq", "z", "x")

    def major(a, step):
        return lax.ppermute(a, along, ring(step, True))

    def minor(a, step):
        return lax.ppermute(a, along, ring(step, False))

    def across(a, step):
        return lax.ppermute(a, "dir", [(i, (i + step) % 4) for i in range(4)])

    def compute():
        p2hi, p2lo, q1f, q1n, qmf, qmn, own = lead(positions, signal, weights)
        table = steer(directions)
        block, three = shaped(K, 2 * COLS), shaped(3, K, 2 * COLS)
        rhi, rlo = major(p2hi, -1), major(p2lo, 1)
        up_far = major(q1f, 1)
        wmf, wmn = call(merge_down_kernel, [block, three], qmf, qmn, rhi)
        down_far = major(wmf, -1)
        down_near = major(wmn, -1)
        (w1n,) = call(merge_up_kernel, [three], q1n, rlo)
        up_near = major(w1n, 1)
        (far,) = call(sum_far_kernel, [block], own, up_far, down_far)
        t2 = minor(far, 2)
        u1, um, s0 = call(
            sum_near_kernel,
            [block, block, shaped(K, 2 * COLS, dtype=F32)],
            own, up_near, down_near,
        )
        v1, v_m = minor(u1, 1), minor(um, -1)
        (zz,) = call(total_kernel, [block], s0, t2, v1, v_m)
        y1, ym, y2 = across(zz, 1), across(zz, -1), across(zz, 2)
        shape = (2, 1, directions.shape[2], signal.shape[2] * 4)
        result = beams((0,), table, (zz,), None, shape)
        result = beams((3, 1), table, (y1, ym), result, shape)
        return beams((2,), table, (y2,), result, shape)

    return compute()


def solution(mesh):
    split = Mesh(mesh.devices.reshape(2, 4, 4, 4), ("freq", "dir", "z", "x"))
    ap = ("z", "x")
    in_specs = (P(None, ap, ("freq", "dir")), P(None, ap), P(), P(None, ap, "dir"))
    out_specs = P(None, ap, "dir", "freq")
    return jax.shard_map(
        local, mesh=split, in_specs=in_specs, out_specs=out_specs, check_vma=False
    )
```

profile of v0, /device:TPU:0, one launch (start us, length us, event | category | flops | bytes accessed | tf_op | source)
XLA Modules:
  0.0 71.8 jit_solution(9347035383565784441)
XLA Ops:
  0.0 10.6 %lead.1 = (bf16[2,256,512]{2,1,0:T(8,128)(2,1)S(1)}, bf16[2,256,512]{2,1,0:T(8,128)(2,1)S(1)}, bf16[16,512,512]{2,1,0:T(8,128)(2,1)S(1)}, bf16[1024,512]{1,0:T(8,128)(2,1)S(1)}, bf16[4,512,512]{2,1,0:T(8,128)(2,1)S(1)}) custom-call(s32[2,4096]{1,0:T(2,128)} %pos_hbm.1, bf16[2,4096,256]{2,1,0:T(8,128)(2,1)} %sig_hbm.1, bf16[4,2,2,2,256,256]{5,4,3,2,1,0:T(8,128)(2,1)} %w_hbm.1), custom_call_target="tpu_custom_call" | custom-call | flops 8000000000 | bytes 12582912 | tf_op jit(solution)/shard_map/lead/pallas_call | solution.py:247
  10.6 4.2 %collective-permute-start.2 = (bf16[2,256,512]{2,1,0:T(8,128)(2,1)S(1)}, bf16[2,256,512]{2,1,0:T(8,128)(2,1)S(1)}, u32[]{:S(2)}, u32[]{:S(2)}) collective-permute-start(bf16[2,256,512]{2,1,0:T(8,128)(2,1)S(1)} %get-tuple-element.28), channel_id=1, source_target_pairs={{0,12},{64,67},{1,13},{65,64},{2,14},{66,65},{3,15},{67,66},{4,0},... | collective-permute-start | bytes 1572872 | tf_op jit(solution)/shard_map/ppermute | solution.py:432
  14.8 3.4 %rest.1 = (bf16[256,512]{1,0:T(8,128)(2,1)S(1)}, bf16[3,256,512]{2,1,0:T(8,128)(2,1)S(1)}, bf16[256,512]{1,0:T(8,128)(2,1)S(1)}, bf16[3,256,512]{2,1,0:T(8,128)(2,1)S(1)}, bf16[4,256,512]{2,1,0:T(8,128)(2,1)S(1)}) custom-call(bf16[16,512,512]{2,1,0:T(8,128)(2,1)S(1)} %get-tuple-element.20.d, bf16[1024,512]{1,0:T(8,128)(2,1)S(1)} %get-tuple-element.21.w43, ...), custom_call_target="tpu_custom_call" | custom-call | flops 3000000000 | bytes 12582912 | tf_op jit(solution)/shard_map/rest/pallas_call | solution.py:273
  18.2 3.3 %collective-permute-done.2.received = bf16[2,256,512]{2,1,0:T(8,128)(2,1)S(1)} collective-permute-done((bf16[2,256,512]{2,1,0:T(8,128)(2,1)S(1)}, bf16[2,256,512]{2,1,0:T(8,128)(2,1)S(1)}, u32[]{:S(2)}, u32[]{:S(2)}) %collective-permute-start.2) | collective-permute-done | bytes 524320 | tf_op jit(solution)/shard_map/ppermute | solution.py:432
  21.5 0.1 shard_map.47
  21.6 3.9 %collective-permute-start.3 = (bf16[3,256,512]{2,1,0:T(8,128)(2,1)S(1)}, bf16[3,256,512]{2,1,0:T(8,128)(2,1)S(1)}, u32[]{:S(2)}, u32[]{:S(2)}) collective-permute-start(bf16[3,256,512]{2,1,0:T(8,128)(2,1)S(1)} %get-tuple-element.29), channel_id=1, source_target_pairs={{0,12},{64,67},{1,13},{65,64},{2,14},{66,65},{3,15},{67,66},{4,0},... | collective-permute-start | bytes 2359304 | tf_op jit(solution)/shard_map/ppermute | solution.py:432
  25.6 0.1 shard_map.46
  25.9 3.2 %collective-permute-start.5 = (bf16[256,512]{1,0:T(8,128)(2,1)S(1)}, bf16[256,512]{1,0:T(8,128)(2,1)S(1)}, u32[]{:S(2)}, u32[]{:S(2)}) collective-permute-start(bf16[256,512]{1,0:T(8,128)(2,1)S(1)} %get-tuple-element.32), channel_id=1, source_target_pairs={{0,12},{64,67},{1,13},{65,64},{2,14},{66,65},{3,15},{67,66},{4,0},... | collective-permute-start | bytes 786440 | tf_op jit(solution)/shard_map/ppermute | solution.py:432
  29.1 12.7 %collective-permute-done.4.up = bf16[256,512]{1,0:T(8,128)(2,1)S(1)} collective-permute-done((bf16[256,512]{1,0:T(8,128)(2,1)S(1)}, bf16[256,512]{1,0:T(8,128)(2,1)S(1)}, u32[]{:S(2)}, u32[]{:S(2)}) %collective-permute-start.4) | collective-permute-done | bytes 262176 | tf_op jit(solution)/shard_map/ppermute | solution.py:432
  41.9 7.6 %collective-permute-start.6 = (bf16[256,512]{1,0:T(8,128)(2,1)S(1)}, bf16[256,512]{1,0:T(8,128)(2,1)S(1)}, u32[]{:S(2)}, u32[]{:S(2)}) collective-permute-start(bf16[256,512]{1,0:T(8,128)(2,1)S(1)} %shard_map.49), channel_id=1, source_target_pairs={{0,2},{64,72},{1,3},{65,73},{2,0},{66,74},{3,1},{67,75},{4,6},{68,... | collective-permute-start | bytes 786440 | tf_op jit(solution)/shard_map/ppermute | solution.py:435
  49.5 0.3 shard_map.48
  49.8 0.6 collective-permute-start.7
  50.3 2.7 %collective-permute-start.8 = (bf16[256,512]{1,0:T(8,128)(2,1)S(1)}, bf16[256,512]{1,0:T(8,128)(2,1)S(1)}, u32[]{:S(2)}, u32[]{:S(2)}) collective-permute-start(bf16[256,512]{1,0:T(8,128)(2,1)S(1)} %get-tuple-element.34), channel_id=1, source_target_pairs={{0,3},{64,76},{1,0},{65,77},{2,1},{66,78},{3,2},{67,79},{4,7},{68,... | collective-permute-start | bytes 786440 | tf_op jit(solution)/shard_map/ppermute | solution.py:435
  53.1 0.8 %collective-permute-done.6.t2 = bf16[256,512]{1,0:T(8,128)(2,1)S(1)} collective-permute-done((bf16[256,512]{1,0:T(8,128)(2,1)S(1)}, bf16[256,512]{1,0:T(8,128)(2,1)S(1)}, u32[]{:S(2)}, u32[]{:S(2)}) %collective-permute-start.6) | collective-permute-done | bytes 262176 | tf_op jit(solution)/shard_map/ppermute | solution.py:435
  53.8 3.6 %collective-permute-done.7.v1 = bf16[256,512]{1,0:T(8,128)(2,1)S(1)} collective-permute-done((bf16[256,512]{1,0:T(8,128)(2,1)S(1)}, bf16[256,512]{1,0:T(8,128)(2,1)S(1)}, u32[]{:S(2)}, u32[]{:S(2)}) %collective-permute-start.7) | collective-permute-done | bytes 262176 | tf_op jit(solution)/shard_map/ppermute | solution.py:435
  57.4 0.1 shard_map.50.refs_1_
  57.5 1.6 %collective-permute-start.10 = (bf16[256,512]{1,0:T(8,128)(2,1)S(1)}, bf16[256,512]{1,0:T(8,128)(2,1)S(1)}, u32[]{:S(2)}, u32[]{:S(2)}) collective-permute-start(bf16[256,512]{1,0:T(8,128)(2,1)S(1)} %shard_map.50.refs_1_), channel_id=1, source_target_pairs={{0,16},{16,32},{32,48},{48,0},{1,17},{17,33},{33,49},{49,1},{2,18}... | collective-permute-start | bytes 786440 | tf_op jit(solution)/shard_map/ppermute | solution.py:438
  59.2 1.7 %collective-permute-start.11 = (bf16[256,512]{1,0:T(8,128)(2,1)S(1)}, bf16[256,512]{1,0:T(8,128)(2,1)S(1)}, u32[]{:S(2)}, u32[]{:S(2)}) collective-permute-start(bf16[256,512]{1,0:T(8,128)(2,1)S(1)} %shard_map.50.refs_1_), channel_id=1, source_target_pairs={{0,48},{16,0},{32,16},{48,32},{1,49},{17,1},{33,17},{49,33},{2,50}... | collective-permute-start | bytes 786440 | tf_op jit(solution)/shard_map/ppermute | solution.py:438
  60.8 1.2 %steer.1.refs_0_ = bf16[1024,512]{1,0:T(8,128)(2,1)S(1)} custom-call(s32[2,1,1024]{2,1,0:T(1,128)S(1)} %copy-done), custom_call_target="tpu_custom_call" | custom-call | flops 1500000000 | bytes 1048576 | tf_op jit(solution)/shard_map/steer/pallas_call | solution.py:310
  62.0 2.1 %collective-permute-start.9 = (bf16[256,512]{1,0:T(8,128)(2,1)S(1)}, bf16[256,512]{1,0:T(8,128)(2,1)S(1)}, u32[]{:S(2)}, u32[]{:S(2)}) collective-permute-start(bf16[256,512]{1,0:T(8,128)(2,1)S(1)} %shard_map.50.refs_1_), channel_id=1, source_target_pairs={{0,32},{16,48},{32,0},{48,16},{1,33},{17,49},{33,1},{49,17},{2,34}... | collective-permute-start | bytes 786440 | tf_op jit(solution)/shard_map/ppermute | solution.py:438
  64.1 1.7 %beams.3.refs_3_ = bf16[2,1,1024,1024]{3,2,1,0:T(8,128)(2,1)} custom-call(bf16[1024,512]{1,0:T(8,128)(2,1)S(1)} %steer.1.refs_0_, bf16[256,512]{1,0:T(8,128)(2,1)S(1)} %shard_map.50.refs_1_), custom_call_target="tpu_custom_call" | custom-call | flops 2000000000 | bytes 1048576 | tf_op jit(solution)/shard_map/beams/pallas_call | solution.py:398
  65.8 2.9 %beams.4.refs_2_ = bf16[2,1,1024,1024]{3,2,1,0:T(8,128)(2,1)} custom-call(bf16[1024,512]{1,0:T(8,128)(2,1)S(1)} %steer.1.refs_0_, bf16[256,512]{1,0:T(8,128)(2,1)S(1)} %collective-permute-done.10.refs_1_, bf16[256,512]{1,0:T(8,128)(2,1)S(1)} %collective-permute-done.11.refs_2_, bf16[2,1,1024,1024]{3,2,1,0:T(8,128)(2,1)} %beams.3.refs_3_), custom_call_target="tpu_custom_call", output_to_operand_aliasing={{}: (3, {})} | custom-call | flops 2000000000 | bytes 1048576 | tf_op jit(solution)/shard_map/beams/pallas_call | solution.py:398
  68.7 1.3 %collective-permute-done.9.refs_1_ = bf16[256,512]{1,0:T(8,128)(2,1)S(1)} collective-permute-done((bf16[256,512]{1,0:T(8,128)(2,1)S(1)}, bf16[256,512]{1,0:T(8,128)(2,1)S(1)}, u32[]{:S(2)}, u32[]{:S(2)}) %collective-permute-start.9) | collective-permute-done | bytes 262176 | tf_op jit(solution)/shard_map/ppermute | solution.py:438
  70.0 1.7 %beams.5 = bf16[2,1,1024,1024]{3,2,1,0:T(8,128)(2,1)} custom-call(bf16[1024,512]{1,0:T(8,128)(2,1)S(1)} %steer.1.refs_0_, bf16[256,512]{1,0:T(8,128)(2,1)S(1)} %collective-permute-done.9.refs_1_, bf16[2,1,1024,1024]{3,2,1,0:T(8,128)(2,1)} %beams.4.refs_2_), custom_call_target="tpu_custom_call", output_to_operand_aliasing={{}: (2, {})} | custom-call | flops 2000000000 | bytes 1048576 | tf_op jit(solution)/shard_map/beams/pallas_call | solution.py:398
  (13 shorter events, 0.3 us)
Async XLA Ops:
  10.6 10.9 %collective-permute-start.2 = (bf16[2,256,512]{2,1,0:T(8,128)(2,1)S(1)}, bf16[2,256,512]{2,1,0:T(8,128)(2,1)S(1)}, u32[]{:S(2)}, u32[]{:S(2)}) collective-permute-start(bf16[2,256,512]{2,1,0:T(8,128)(2,1)S(1)} %get-tuple-element.28), channel_id=1, source_target_pairs={{0,12},{64,67},{1,13},{65,64},{2,14},{66,65},{3,15},{67,66},{4,0},... | collective-permute-start | bytes 1572872 | tf_op jit(solution)/shard_map/ppermute | solution.py:432
  14.8 10.8 %collective-permute-start = (bf16[2,256,512]{2,1,0:T(8,128)(2,1)S(1)}, bf16[2,256,512]{2,1,0:T(8,128)(2,1)S(1)}, u32[]{:S(2)}, u32[]{:S(2)}) collective-permute-start(bf16[2,256,512]{2,1,0:T(8,128)(2,1)S(1)} %get-tuple-element.25), channel_id=1, source_target_pairs={{0,4},{64,65},{1,5},{65,66},{2,6},{66,67},{3,7},{67,64},{4,8},{68,... | collective-permute-start | bytes 1572872 | tf_op jit(solution)/shard_map/ppermute | solution.py:432
  21.6 39.2 %copy-start = (s32[2,1,1024]{2,1,0:T(1,128)S(1)}, s32[2,1,1024]{2,1,0:T(1,128)}, u32[]{:S(2)}) copy-start(s32[2,1,1024]{2,1,0:T(1,128)} %pos.1) | copy-start | bytes 24580
  21.6 27.8 %collective-permute-start.3 = (bf16[3,256,512]{2,1,0:T(8,128)(2,1)S(1)}, bf16[3,256,512]{2,1,0:T(8,128)(2,1)S(1)}, u32[]{:S(2)}, u32[]{:S(2)}) collective-permute-start(bf16[3,256,512]{2,1,0:T(8,128)(2,1)S(1)} %get-tuple-element.29), channel_id=1, source_target_pairs={{0,12},{64,67},{1,13},{65,64},{2,14},{66,65},{3,15},{67,66},{4,0},... | collective-permute-start | bytes 2359304 | tf_op jit(solution)/shard_map/ppermute | solution.py:432
  25.7 23.8 %collective-permute-start.1 = (bf16[3,256,512]{2,1,0:T(8,128)(2,1)S(1)}, bf16[3,256,512]{2,1,0:T(8,128)(2,1)S(1)}, u32[]{:S(2)}, u32[]{:S(2)}) collective-permute-start(bf16[3,256,512]{2,1,0:T(8,128)(2,1)S(1)} %shard_map.46), channel_id=1, source_target_pairs={{0,4},{64,65},{1,5},{65,66},{2,6},{66,67},{3,7},{67,64},{4,8},{68,... | collective-permute-start | bytes 2359304 | tf_op jit(solution)/shard_map/ppermute | solution.py:432
  25.8 16.0 %collective-permute-start.4 = (bf16[256,512]{1,0:T(8,128)(2,1)S(1)}, bf16[256,512]{1,0:T(8,128)(2,1)S(1)}, u32[]{:S(2)}, u32[]{:S(2)}) collective-permute-start(bf16[256,512]{1,0:T(8,128)(2,1)S(1)} %get-tuple-element.31), channel_id=1, source_target_pairs={{0,4},{64,65},{1,5},{65,66},{2,6},{66,67},{3,7},{67,64},{4,8},{68,... | collective-permute-start | bytes 786440 | tf_op jit(solution)/shard_map/ppermute | solution.py:432
  25.9 15.9 %collective-permute-start.5 = (bf16[256,512]{1,0:T(8,128)(2,1)S(1)}, bf16[256,512]{1,0:T(8,128)(2,1)S(1)}, u32[]{:S(2)}, u32[]{:S(2)}) collective-permute-start(bf16[256,512]{1,0:T(8,128)(2,1)S(1)} %get-tuple-element.32), channel_id=1, source_target_pairs={{0,12},{64,67},{1,13},{65,64},{2,14},{66,65},{3,15},{67,66},{4,0},... | collective-permute-start | bytes 786440 | tf_op jit(solution)/shard_map/ppermute | solution.py:432
  41.9 11.9 %collective-permute-start.6 = (bf16[256,512]{1,0:T(8,128)(2,1)S(1)}, bf16[256,512]{1,0:T(8,128)(2,1)S(1)}, u32[]{:S(2)}, u32[]{:S(2)}) collective-permute-start(bf16[256,512]{1,0:T(8,128)(2,1)S(1)} %shard_map.49), channel_id=1, source_target_pairs={{0,2},{64,72},{1,3},{65,73},{2,0},{66,74},{3,1},{67,75},{4,6},{68,... | collective-permute-start | bytes 786440 | tf_op jit(solution)/shard_map/ppermute | solution.py:435
  49.8 7.7 %collective-permute-start.7 = (bf16[256,512]{1,0:T(8,128)(2,1)S(1)}, bf16[256,512]{1,0:T(8,128)(2,1)S(1)}, u32[]{:S(2)}, u32[]{:S(2)}) collective-permute-start(bf16[256,512]{1,0:T(8,128)(2,1)S(1)} %get-tuple-element.33), channel_id=1, source_target_pairs={{0,1},{64,68},{1,2},{65,69},{2,3},{66,70},{3,0},{67,71},{4,5},{68,... | collective-permute-start | bytes 786440 | tf_op jit(solution)/shard_map/ppermute | solution.py:435
  50.3 7.1 %collective-permute-start.8 = (bf16[256,512]{1,0:T(8,128)(2,1)S(1)}, bf16[256,512]{1,0:T(8,128)(2,1)S(1)}, u32[]{:S(2)}, u32[]{:S(2)}) collective-permute-start(bf16[256,512]{1,0:T(8,128)(2,1)S(1)} %get-tuple-element.34), channel_id=1, source_target_pairs={{0,3},{64,76},{1,0},{65,77},{2,1},{66,78},{3,2},{67,79},{4,7},{68,... | collective-permute-start | bytes 786440 | tf_op jit(solution)/shard_map/ppermute | solution.py:435
  57.5 8.2 %collective-permute-start.10 = (bf16[256,512]{1,0:T(8,128)(2,1)S(1)}, bf16[256,512]{1,0:T(8,128)(2,1)S(1)}, u32[]{:S(2)}, u32[]{:S(2)}) collective-permute-start(bf16[256,512]{1,0:T(8,128)(2,1)S(1)} %shard_map.50.refs_1_), channel_id=1, source_target_pairs={{0,16},{16,32},{32,48},{48,0},{1,17},{17,33},{33,49},{49,1},{2,18}... | collective-permute-start | bytes 786440 | tf_op jit(solution)/shard_map/ppermute | solution.py:438
  59.2 6.6 %collective-permute-start.11 = (bf16[256,512]{1,0:T(8,128)(2,1)S(1)}, bf16[256,512]{1,0:T(8,128)(2,1)S(1)}, u32[]{:S(2)}, u32[]{:S(2)}) collective-permute-start(bf16[256,512]{1,0:T(8,128)(2,1)S(1)} %shard_map.50.refs_1_), channel_id=1, source_target_pairs={{0,48},{16,0},{32,16},{48,32},{1,49},{17,1},{33,17},{49,33},{2,50}... | collective-permute-start | bytes 786440 | tf_op jit(solution)/shard_map/ppermute | solution.py:438
  62.0 8.0 %collective-permute-start.9 = (bf16[256,512]{1,0:T(8,128)(2,1)S(1)}, bf16[256,512]{1,0:T(8,128)(2,1)S(1)}, u32[]{:S(2)}, u32[]{:S(2)}) collective-permute-start(bf16[256,512]{1,0:T(8,128)(2,1)S(1)} %shard_map.50.refs_1_), channel_id=1, source_target_pairs={{0,32},{16,48},{32,0},{48,16},{1,33},{17,49},{33,1},{49,17},{2,34}... | collective-permute-start | bytes 786440 | tf_op jit(solution)/shard_map/ppermute | solution.py:438
where the time goes:
time: 72.2 us; the launch traced here: 71.8 us
  starting transfers between devices  27.8 us (39%)
  Pallas kernels  22.2 us (31%)
  waiting for transfers between devices  21.6 us (30%)
    ppermute x6, waiting for transfers between devices, major(): return lax.ppermute(a, along, ring(step, True))  16 us
    ppermute x6, starting transfers between devices, major(): return lax.ppermute(a, along, ring(step, True))  11.5 us
    ppermute x3, starting transfers between devices, minor(): return lax.ppermute(a, along, ring(step, False))  10.9 us
    pallas_call x1, Pallas kernels, lead(): pl.pallas_call(lead_kernel, out_shape=[shaped(2, K, 2 * COLS)] * 2 + [sha...  10.6 us
    pallas_call x3, Pallas kernels, beams(): pl.pallas_call(lambda *refs: beam_kernel(offsets, *refs), out_shape=jax.S...  6.24 us
    ppermute x3, starting transfers between devices, across(): return lax.ppermute(a, 'dir', [(i, (i + step) % 4) for i in range(4)])  5.37 us
    ppermute x3, waiting for transfers between devices, minor(): return lax.ppermute(a, along, ring(step, False))  4.35 us
    pallas_call x1, Pallas kernels, lead(): pl.pallas_call(rest_kernel, out_shape=[shaped(*n, K, 2 * COLS) for n in (...  3.43 us
  transfers between devices with their start and end apart: 12, of which 5 were waited for; matrix products, arithmetic and copies ran while one was open for 0% of the time, Pallas kernels for 14%

commit v1 on v0

--- a/solution.py
+++ b/solution.py
@@ -349,18 +349,25 @@
     out_near[1:3] = added(near[1:3], received[...]).astype(BF)
 
 
-def sum_far_kernel(own, up, down, out):
-    out[...] = added(own[0], up[...], down[...]).astype(BF)
-
-
-def sum_near_kernel(own, up, down, u1, um, s0):
-    u1[...] = added(own[1], up[0], down[0]).astype(BF)
-    um[...] = added(own[2], up[1], down[1]).astype(BF)
+def sum_far_kernel(own, up, down, lo, hi):
+    s = added(own[0], up[...], down[...]).astype(BF)
+    lo[...] = s[: K // 2]
+    hi[...] = s[K // 2 :]
+
+
+def sum_near_kernel(own, up, down, tlo, thi, u1, um, s0):
+    h = K // 2
+    one = added(own[1], up[0], down[0])
+    u1[0:h] = (one[:h] + tlo[...].astype(F32)).astype(BF)
+    u1[h:] = one[h:].astype(BF)
+    other = added(own[2], up[1], down[1])
+    um[0:h] = other[:h].astype(BF)
+    um[h:] = (other[h:] + thi[...].astype(F32)).astype(BF)
     s0[...] = added(own[3], up[2], down[2])
 
 
-def total_kernel(s0, t2, v1, v_m, z):
-    z[...] = added(s0[...], t2[...], v1[...], v_m[...]).astype(BF)
+def total_kernel(s0, v1, v_m, z):
+    z[...] = added(s0[...], v1[...], v_m[...]).astype(BF)
 
 
 def beam_kernel(offsets, table, *rest):
@@ -448,15 +455,16 @@
         down_near = major(wmn, -1)
         (w1n,) = call(merge_up_kernel, [three], q1n, rlo)
         up_near = major(w1n, 1)
-        (far,) = call(sum_far_kernel, [block], own, up_far, down_far)
-        t2 = minor(far, 2)
+        half = shaped(K // 2, 2 * COLS)
+        lo, hi = call(sum_far_kernel, [half, half], own, up_far, down_far)
+        tlo, thi = minor(lo, 1), minor(hi, -1)
         u1, um, s0 = call(
             sum_near_kernel,
             [block, block, shaped(K, 2 * COLS, dtype=F32)],
-            own, up_near, down_near,
+            own, up_near, down_near, tlo, thi,
         )
         v1, v_m = minor(u1, 1), minor(um, -1)
-        (zz,) = call(total_kernel, [block], s0, t2, v1, v_m)
+        (zz,) = call(total_kernel, [block], s0, v1, v_m)
         y1, ym, y2 = across(zz, 1), across(zz, -1), across(zz, 2)
         shape = (2, 1, directions.shape[2], signal.shape[2] * 4)
         result = beams((0,), table, (zz,), None, shape)

time: 72.2 us -> 72.5 us (level)
  waiting for transfers between devices: 21.6 us -> 25.8 us
  starting transfers between devices: 27.8 us -> 24.2 us
    ppermute x3 -> x4, waiting for transfers between devices: 4.35 us -> 8.6 us  [minor(): return lax.ppermute(a, along, ring(step, False))]
    ppermute x3 -> x4, starting transfers between devices: 10.9 us -> 7.27 us  [minor(): return lax.ppermute(a, along, ring(step, False))]
  transfers between devices with their start and end apart: 12 -> 13, of which waited for: 5 -> 7; matrix products, arithmetic and copies ran while one was open for 0% -> 0% of each run, Pallas kernels for 14% -> 13%
where the time goes in v1:
time: 72.5 us; the launch traced here: 72.4 us
  waiting for transfers between devices  25.8 us (36%)
  starting transfers between devices  24.2 us (33%)
  Pallas kernels  22.2 us (31%)
    ppermute x6, waiting for transfers between devices, major(): return lax.ppermute(a, along, ring(step, True))  16 us
    ppermute x6, starting transfers between devices, major(): return lax.ppermute(a, along, ring(step, True))  11.5 us
    pallas_call x1, Pallas kernels, lead(): pl.pallas_call(lead_kernel, out_shape=[shaped(2, K, 2 * COLS)] * 2 + [sha...  10.6 us
    ppermute x4, waiting for transfers between devices, minor(): return lax.ppermute(a, along, ring(step, False))  8.6 us
    ppermute x4, starting transfers between devices, minor(): return lax.ppermute(a, along, ring(step, False))  7.27 us
    pallas_call x3, Pallas kernels, beams(): pl.pallas_call(lambda *refs: beam_kernel(offsets, *refs), out_shape=jax.S...  6.24 us
    ppermute x3, starting transfers between devices, across(): return lax.ppermute(a, 'dir', [(i, (i + step) % 4) for i in range(4)])  5.37 us
    pallas_call x1, Pallas kernels, lead(): pl.pallas_call(rest_kernel, out_shape=[shaped(*n, K, 2 * COLS) for n in (...  3.43 us
  transfers between devices with their start and end apart: 13, of which 7 were waited for; matrix products, arithmetic and copies ran while one was open for 0% of the time, Pallas kernels for 13%

profile of v1, /device:TPU:0, one launch (start us, length us, event | category | flops | bytes accessed | tf_op | source)
XLA Modules:
  0.0 72.4 jit_solution(2839384842746493886)
XLA Ops:
  0.0 10.6 %lead.1 = (bf16[2,256,512]{2,1,0:T(8,128)(2,1)S(1)}, bf16[2,256,512]{2,1,0:T(8,128)(2,1)S(1)}, bf16[16,512,512]{2,1,0:T(8,128)(2,1)S(1)}, bf16[1024,512]{1,0:T(8,128)(2,1)S(1)}, bf16[4,512,512]{2,1,0:T(8,128)(2,1)S(1)}) custom-call(s32[2,4096]{1,0:T(2,128)} %pos_hbm.1, bf16[2,4096,256]{2,1,0:T(8,128)(2,1)} %sig_hbm.1, bf16[4,2,2,2,256,256]{5,4,3,2,1,0:T(8,128)(2,1)} %w_hbm.1), custom_call_target="tpu_custom_call" | custom-call | flops 8000000000 | bytes 12582912 | tf_op jit(solution)/shard_map/lead/pallas_call | solution.py:247
  10.6 4.2 %collective-permute-start.2 = (bf16[2,256,512]{2,1,0:T(8,128)(2,1)S(1)}, bf16[2,256,512]{2,1,0:T(8,128)(2,1)S(1)}, u32[]{:S(2)}, u32[]{:S(2)}) collective-permute-start(bf16[2,256,512]{2,1,0:T(8,128)(2,1)S(1)} %get-tuple-element.30), channel_id=1, source_target_pairs={{0,12},{64,67},{1,13},{65,64},{2,14},{66,65},{3,15},{67,66},{4,0},... | collective-permute-start | bytes 1572872 | tf_op jit(solution)/shard_map/ppermute | solution.py:439
  14.8 3.4 %rest.1 = (bf16[256,512]{1,0:T(8,128)(2,1)S(1)}, bf16[3,256,512]{2,1,0:T(8,128)(2,1)S(1)}, bf16[256,512]{1,0:T(8,128)(2,1)S(1)}, bf16[3,256,512]{2,1,0:T(8,128)(2,1)S(1)}, bf16[4,256,512]{2,1,0:T(8,128)(2,1)S(1)}) custom-call(bf16[16,512,512]{2,1,0:T(8,128)(2,1)S(1)} %get-tuple-element.22.d, bf16[1024,512]{1,0:T(8,128)(2,1)S(1)} %get-tuple-element.23.w43, ...), custom_call_target="tpu_custom_call" | custom-call | flops 3000000000 | bytes 12582912 | tf_op jit(solution)/shard_map/rest/pallas_call | solution.py:273
  18.2 3.3 %collective-permute-done.2.received = bf16[2,256,512]{2,1,0:T(8,128)(2,1)S(1)} collective-permute-done((bf16[2,256,512]{2,1,0:T(8,128)(2,1)S(1)}, bf16[2,256,512]{2,1,0:T(8,128)(2,1)S(1)}, u32[]{:S(2)}, u32[]{:S(2)}) %collective-permute-start.2) | collective-permute-done | bytes 524320 | tf_op jit(solution)/shard_map/ppermute | solution.py:439
  21.6 3.9 %collective-permute-start.3 = (bf16[3,256,512]{2,1,0:T(8,128)(2,1)S(1)}, bf16[3,256,512]{2,1,0:T(8,128)(2,1)S(1)}, u32[]{:S(2)}, u32[]{:S(2)}) collective-permute-start(bf16[3,256,512]{2,1,0:T(8,128)(2,1)S(1)} %get-tuple-element.31), channel_id=1, source_target_pairs={{0,12},{64,67},{1,13},{65,64},{2,14},{66,65},{3,15},{67,66},{4,0},... | collective-permute-start | bytes 2359304 | tf_op jit(solution)/shard_map/ppermute | solution.py:439
  25.9 3.2 %collective-permute-start.5 = (bf16[256,512]{1,0:T(8,128)(2,1)S(1)}, bf16[256,512]{1,0:T(8,128)(2,1)S(1)}, u32[]{:S(2)}, u32[]{:S(2)}) collective-permute-start(bf16[256,512]{1,0:T(8,128)(2,1)S(1)} %get-tuple-element.33), channel_id=1, source_target_pairs={{0,12},{64,67},{1,13},{65,64},{2,14},{66,65},{3,15},{67,66},{4,0},... | collective-permute-start | bytes 786440 | tf_op jit(solution)/shard_map/ppermute | solution.py:439
  29.1 12.7 %collective-permute-done.4.up = bf16[256,512]{1,0:T(8,128)(2,1)S(1)} collective-permute-done((bf16[256,512]{1,0:T(8,128)(2,1)S(1)}, bf16[256,512]{1,0:T(8,128)(2,1)S(1)}, u32[]{:S(2)}, u32[]{:S(2)}) %collective-permute-start.4) | collective-permute-done | bytes 262176 | tf_op jit(solution)/shard_map/ppermute | solution.py:439
  41.9 2.3 %collective-permute-start.6 = (bf16[128,512]{1,0:T(8,128)(2,1)S(1)}, bf16[128,512]{1,0:T(8,128)(2,1)S(1)}, u32[]{:S(2)}, u32[]{:S(2)}) collective-permute-start(bf16[128,512]{1,0:T(8,128)(2,1)S(1)} %get-tuple-element.34), channel_id=1, source_target_pairs={{0,1},{64,68},{1,2},{65,69},{2,3},{66,70},{3,0},{67,71},{4,5},{68,... | collective-permute-start | bytes 393224 | tf_op jit(solution)/shard_map/ppermute | solution.py:442
  44.2 1.6 %collective-permute-start.7 = (bf16[128,512]{1,0:T(8,128)(2,1)S(1)}, bf16[128,512]{1,0:T(8,128)(2,1)S(1)}, u32[]{:S(2)}, u32[]{:S(2)}) collective-permute-start(bf16[128,512]{1,0:T(8,128)(2,1)S(1)} %get-tuple-element.35), channel_id=1, source_target_pairs={{0,3},{64,76},{1,0},{65,77},{2,1},{66,78},{3,2},{67,79},{4,7},{68,... | collective-permute-start | bytes 393224 | tf_op jit(solution)/shard_map/ppermute | solution.py:442
  45.9 2.9 %collective-permute-done.6.tlo = bf16[128,512]{1,0:T(8,128)(2,1)S(1)} collective-permute-done((bf16[128,512]{1,0:T(8,128)(2,1)S(1)}, bf16[128,512]{1,0:T(8,128)(2,1)S(1)}, u32[]{:S(2)}, u32[]{:S(2)}) %collective-permute-start.6) | collective-permute-done | bytes 131104 | tf_op jit(solution)/shard_map/ppermute | solution.py:442
  48.7 0.6 collective-permute-done.7.thi
  49.3 0.3 shard_map.49
  49.6 2.1 %collective-permute-start.8 = (bf16[256,512]{1,0:T(8,128)(2,1)S(1)}, bf16[256,512]{1,0:T(8,128)(2,1)S(1)}, u32[]{:S(2)}, u32[]{:S(2)}) collective-permute-start(bf16[256,512]{1,0:T(8,128)(2,1)S(1)} %get-tuple-element.37), channel_id=1, source_target_pairs={{0,1},{64,68},{1,2},{65,69},{2,3},{66,70},{3,0},{67,71},{4,5},{68,... | collective-permute-start | bytes 786440 | tf_op jit(solution)/shard_map/ppermute | solution.py:442
  51.7 1.2 %collective-permute-start.9 = (bf16[256,512]{1,0:T(8,128)(2,1)S(1)}, bf16[256,512]{1,0:T(8,128)(2,1)S(1)}, u32[]{:S(2)}, u32[]{:S(2)}) collective-permute-start(bf16[256,512]{1,0:T(8,128)(2,1)S(1)} %get-tuple-element.38), channel_id=1, source_target_pairs={{0,3},{64,76},{1,0},{65,77},{2,1},{66,78},{3,2},{67,79},{4,7},{68,... | collective-permute-start | bytes 786440 | tf_op jit(solution)/shard_map/ppermute | solution.py:442
  52.9 4.3 %collective-permute-done.8.v1 = bf16[256,512]{1,0:T(8,128)(2,1)S(1)} collective-permute-done((bf16[256,512]{1,0:T(8,128)(2,1)S(1)}, bf16[256,512]{1,0:T(8,128)(2,1)S(1)}, u32[]{:S(2)}, u32[]{:S(2)}) %collective-permute-start.8) | collective-permute-done | bytes 262176 | tf_op jit(solution)/shard_map/ppermute | solution.py:442
  57.3 0.8 %collective-permute-done.9.v_m = bf16[256,512]{1,0:T(8,128)(2,1)S(1)} collective-permute-done((bf16[256,512]{1,0:T(8,128)(2,1)S(1)}, bf16[256,512]{1,0:T(8,128)(2,1)S(1)}, u32[]{:S(2)}, u32[]{:S(2)}) %collective-permute-start.9) | collective-permute-done | bytes 262176 | tf_op jit(solution)/shard_map/ppermute | solution.py:442
  58.2 1.6 %collective-permute-start.11 = (bf16[256,512]{1,0:T(8,128)(2,1)S(1)}, bf16[256,512]{1,0:T(8,128)(2,1)S(1)}, u32[]{:S(2)}, u32[]{:S(2)}) collective-permute-start(bf16[256,512]{1,0:T(8,128)(2,1)S(1)} %shard_map.50.refs_1_), channel_id=1, source_target_pairs={{0,16},{16,32},{32,48},{48,0},{1,17},{17,33},{33,49},{49,1},{2,18}... | collective-permute-start | bytes 786440 | tf_op jit(solution)/shard_map/ppermute | solution.py:445
  59.8 1.7 %collective-permute-start.12 = (bf16[256,512]{1,0:T(8,128)(2,1)S(1)}, bf16[256,512]{1,0:T(8,128)(2,1)S(1)}, u32[]{:S(2)}, u32[]{:S(2)}) collective-permute-start(bf16[256,512]{1,0:T(8,128)(2,1)S(1)} %shard_map.50.refs_1_), channel_id=1, source_target_pairs={{0,48},{16,0},{32,16},{48,32},{1,49},{17,1},{33,17},{49,33},{2,50}... | collective-permute-start | bytes 786440 | tf_op jit(solution)/shard_map/ppermute | solution.py:445
  61.5 1.2 %steer.1.refs_0_ = bf16[1024,512]{1,0:T(8,128)(2,1)S(1)} custom-call(s32[2,1,1024]{2,1,0:T(1,128)S(1)} %copy-done), custom_call_target="tpu_custom_call" | custom-call | flops 1500000000 | bytes 1048576 | tf_op jit(solution)/shard_map/steer/pallas_call | solution.py:310
  62.7 2.1 %collective-permute-start.10 = (bf16[256,512]{1,0:T(8,128)(2,1)S(1)}, bf16[256,512]{1,0:T(8,128)(2,1)S(1)}, u32[]{:S(2)}, u32[]{:S(2)}) collective-permute-start(bf16[256,512]{1,0:T(8,128)(2,1)S(1)} %shard_map.50.refs_1_), channel_id=1, source_target_pairs={{0,32},{16,48},{32,0},{48,16},{1,33},{17,49},{33,1},{49,17},{2,34}... | collective-permute-start | bytes 786440 | tf_op jit(solution)/shard_map/ppermute | solution.py:445
  64.7 1.7 %beams.3.refs_3_ = bf16[2,1,1024,1024]{3,2,1,0:T(8,128)(2,1)} custom-call(bf16[1024,512]{1,0:T(8,128)(2,1)S(1)} %steer.1.refs_0_, bf16[256,512]{1,0:T(8,128)(2,1)S(1)} %shard_map.50.refs_1_), custom_call_target="tpu_custom_call" | custom-call | flops 2000000000 | bytes 1048576 | tf_op jit(solution)/shard_map/beams/pallas_call | solution.py:405
  66.4 2.9 %beams.4.refs_2_ = bf16[2,1,1024,1024]{3,2,1,0:T(8,128)(2,1)} custom-call(bf16[1024,512]{1,0:T(8,128)(2,1)S(1)} %steer.1.refs_0_, bf16[256,512]{1,0:T(8,128)(2,1)S(1)} %collective-permute-done.11.refs_1_, bf16[256,512]{1,0:T(8,128)(2,1)S(1)} %collective-permute-done.12.refs_2_, bf16[2,1,1024,1024]{3,2,1,0:T(8,128)(2,1)} %beams.3.refs_3_), custom_call_target="tpu_custom_call", output_to_operand_aliasing={{}: (3, {})} | custom-call | flops 2000000000 | bytes 1048576 | tf_op jit(solution)/shard_map/beams/pallas_call | solution.py:405
  69.3 1.3 %collective-permute-done.10.refs_1_ = bf16[256,512]{1,0:T(8,128)(2,1)S(1)} collective-permute-done((bf16[256,512]{1,0:T(8,128)(2,1)S(1)}, bf16[256,512]{1,0:T(8,128)(2,1)S(1)}, u32[]{:S(2)}, u32[]{:S(2)}) %collective-permute-start.10) | collective-permute-done | bytes 262176 | tf_op jit(solution)/shard_map/ppermute | solution.py:445
  70.6 1.7 %beams.5 = bf16[2,1,1024,1024]{3,2,1,0:T(8,128)(2,1)} custom-call(bf16[1024,512]{1,0:T(8,128)(2,1)S(1)} %steer.1.refs_0_, bf16[256,512]{1,0:T(8,128)(2,1)S(1)} %collective-permute-done.10.refs_1_, bf16[2,1,1024,1024]{3,2,1,0:T(8,128)(2,1)} %beams.4.refs_2_), custom_call_target="tpu_custom_call", output_to_operand_aliasing={{}: (2, {})} | custom-call | flops 2000000000 | bytes 1048576 | tf_op jit(solution)/shard_map/beams/pallas_call | solution.py:405
  (15 shorter events, 0.6 us)
Async XLA Ops:
  10.6 10.9 %collective-permute-start.2 = (bf16[2,256,512]{2,1,0:T(8,128)(2,1)S(1)}, bf16[2,256,512]{2,1,0:T(8,128)(2,1)S(1)}, u32[]{:S(2)}, u32[]{:S(2)}) collective-permute-start(bf16[2,256,512]{2,1,0:T(8,128)(2,1)S(1)} %get-tuple-element.30), channel_id=1, source_target_pairs={{0,12},{64,67},{1,13},{65,64},{2,14},{66,65},{3,15},{67,66},{4,0},... | collective-permute-start | bytes 1572872 | tf_op jit(solution)/shard_map/ppermute | solution.py:439
  14.8 10.8 %collective-permute-start = (bf16[2,256,512]{2,1,0:T(8,128)(2,1)S(1)}, bf16[2,256,512]{2,1,0:T(8,128)(2,1)S(1)}, u32[]{:S(2)}, u32[]{:S(2)}) collective-permute-start(bf16[2,256,512]{2,1,0:T(8,128)(2,1)S(1)} %get-tuple-element.27), channel_id=1, source_target_pairs={{0,4},{64,65},{1,5},{65,66},{2,6},{66,67},{3,7},{67,64},{4,8},{68,... | collective-permute-start | bytes 1572872 | tf_op jit(solution)/shard_map/ppermute | solution.py:439
  21.6 39.9 %copy-start = (s32[2,1,1024]{2,1,0:T(1,128)S(1)}, s32[2,1,1024]{2,1,0:T(1,128)}, u32[]{:S(2)}) copy-start(s32[2,1,1024]{2,1,0:T(1,128)} %pos.1) | copy-start | bytes 24580
  21.6 27.7 %collective-permute-start.3 = (bf16[3,256,512]{2,1,0:T(8,128)(2,1)S(1)}, bf16[3,256,512]{2,1,0:T(8,128)(2,1)S(1)}, u32[]{:S(2)}, u32[]{:S(2)}) collective-permute-start(bf16[3,256,512]{2,1,0:T(8,128)(2,1)S(1)} %get-tuple-element.31), channel_id=1, source_target_pairs={{0,12},{64,67},{1,13},{65,64},{2,14},{66,65},{3,15},{67,66},{4,0},... | collective-permute-start | bytes 2359304 | tf_op jit(solution)/shard_map/ppermute | solution.py:439
  25.7 23.6 %collective-permute-start.1 = (bf16[3,256,512]{2,1,0:T(8,128)(2,1)S(1)}, bf16[3,256,512]{2,1,0:T(8,128)(2,1)S(1)}, u32[]{:S(2)}, u32[]{:S(2)}) collective-permute-start(bf16[3,256,512]{2,1,0:T(8,128)(2,1)S(1)} %shard_map.46), channel_id=1, source_target_pairs={{0,4},{64,65},{1,5},{65,66},{2,6},{66,67},{3,7},{67,64},{4,8},{68,... | collective-permute-start | bytes 2359304 | tf_op jit(solution)/shard_map/ppermute | solution.py:439
  25.8 16.0 %collective-permute-start.4 = (bf16[256,512]{1,0:T(8,128)(2,1)S(1)}, bf16[256,512]{1,0:T(8,128)(2,1)S(1)}, u32[]{:S(2)}, u32[]{:S(2)}) collective-permute-start(bf16[256,512]{1,0:T(8,128)(2,1)S(1)} %get-tuple-element.32), channel_id=1, source_target_pairs={{0,4},{64,65},{1,5},{65,66},{2,6},{66,67},{3,7},{67,64},{4,8},{68,... | collective-permute-start | bytes 786440 | tf_op jit(solution)/shard_map/ppermute | solution.py:439
  25.9 15.9 %collective-permute-start.5 = (bf16[256,512]{1,0:T(8,128)(2,1)S(1)}, bf16[256,512]{1,0:T(8,128)(2,1)S(1)}, u32[]{:S(2)}, u32[]{:S(2)}) collective-permute-start(bf16[256,512]{1,0:T(8,128)(2,1)S(1)} %get-tuple-element.33), channel_id=1, source_target_pairs={{0,12},{64,67},{1,13},{65,64},{2,14},{66,65},{3,15},{67,66},{4,0},... | collective-permute-start | bytes 786440 | tf_op jit(solution)/shard_map/ppermute | solution.py:439
  41.9 6.8 %collective-permute-start.6 = (bf16[128,512]{1,0:T(8,128)(2,1)S(1)}, bf16[128,512]{1,0:T(8,128)(2,1)S(1)}, u32[]{:S(2)}, u32[]{:S(2)}) collective-permute-start(bf16[128,512]{1,0:T(8,128)(2,1)S(1)} %get-tuple-element.34), channel_id=1, source_target_pairs={{0,1},{64,68},{1,2},{65,69},{2,3},{66,70},{3,0},{67,71},{4,5},{68,... | collective-permute-start | bytes 393224 | tf_op jit(solution)/shard_map/ppermute | solution.py:442
  44.2 5.1 %collective-permute-start.7 = (bf16[128,512]{1,0:T(8,128)(2,1)S(1)}, bf16[128,512]{1,0:T(8,128)(2,1)S(1)}, u32[]{:S(2)}, u32[]{:S(2)}) collective-permute-start(bf16[128,512]{1,0:T(8,128)(2,1)S(1)} %get-tuple-element.35), channel_id=1, source_target_pairs={{0,3},{64,76},{1,0},{65,77},{2,1},{66,78},{3,2},{67,79},{4,7},{68,... | collective-permute-start | bytes 393224 | tf_op jit(solution)/shard_map/ppermute | solution.py:442
  49.6 7.7 %collective-permute-start.8 = (bf16[256,512]{1,0:T(8,128)(2,1)S(1)}, bf16[256,512]{1,0:T(8,128)(2,1)S(1)}, u32[]{:S(2)}, u32[]{:S(2)}) collective-permute-start(bf16[256,512]{1,0:T(8,128)(2,1)S(1)} %get-tuple-element.37), channel_id=1, source_target_pairs={{0,1},{64,68},{1,2},{65,69},{2,3},{66,70},{3,0},{67,71},{4,5},{68,... | collective-permute-start | bytes 786440 | tf_op jit(solution)/shard_map/ppermute | solution.py:442
  51.7 6.4 %collective-permute-start.9 = (bf16[256,512]{1,0:T(8,128)(2,1)S(1)}, bf16[256,512]{1,0:T(8,128)(2,1)S(1)}, u32[]{:S(2)}, u32[]{:S(2)}) collective-permute-start(bf16[256,512]{1,0:T(8,128)(2,1)S(1)} %get-tuple-element.38), channel_id=1, source_target_pairs={{0,3},{64,76},{1,0},{65,77},{2,1},{66,78},{3,2},{67,79},{4,7},{68,... | collective-permute-start | bytes 786440 | tf_op jit(solution)/shard_map/ppermute | solution.py:442
  58.2 8.2 %collective-permute-start.11 = (bf16[256,512]{1,0:T(8,128)(2,1)S(1)}, bf16[256,512]{1,0:T(8,128)(2,1)S(1)}, u32[]{:S(2)}, u32[]{:S(2)}) collective-permute-start(bf16[256,512]{1,0:T(8,128)(2,1)S(1)} %shard_map.50.refs_1_), channel_id=1, source_target_pairs={{0,16},{16,32},{32,48},{48,0},{1,17},{17,33},{33,49},{49,1},{2,18}... | collective-permute-start | bytes 786440 | tf_op jit(solution)/shard_map/ppermute | solution.py:445
  59.8 6.6 %collective-permute-start.12 = (bf16[256,512]{1,0:T(8,128)(2,1)S(1)}, bf16[256,512]{1,0:T(8,128)(2,1)S(1)}, u32[]{:S(2)}, u32[]{:S(2)}) collective-permute-start(bf16[256,512]{1,0:T(8,128)(2,1)S(1)} %shard_map.50.refs_1_), channel_id=1, source_target_pairs={{0,48},{16,0},{32,16},{48,32},{1,49},{17,1},{33,17},{49,33},{2,50}... | collective-permute-start | bytes 786440 | tf_op jit(solution)/shard_map/ppermute | solution.py:445
  62.7 8.0 %collective-permute-start.10 = (bf16[256,512]{1,0:T(8,128)(2,1)S(1)}, bf16[256,512]{1,0:T(8,128)(2,1)S(1)}, u32[]{:S(2)}, u32[]{:S(2)}) collective-permute-start(bf16[256,512]{1,0:T(8,128)(2,1)S(1)} %shard_map.50.refs_1_), channel_id=1, source_target_pairs={{0,32},{16,48},{32,0},{48,16},{1,33},{17,49},{33,1},{49,17},{2,34}... | collective-permute-start | bytes 786440 | tf_op jit(solution)/shard_map/ppermute | solution.py:445
